TPU v7x, 32 devices: a whole 2x2x4 slice. The times are simulated.
32 devices in a mesh: section: 4 (over z), gx: 2 (over x), gy: 2 (over y), gz: 2 (over core).
Axes of the slice: x: 2, y: 2, z: 4, core: 2. Of those that a mesh axis runs over, the one named last changes fastest.
Arguments:
- micro_inputs: bfloat16 [1, 256, 8192], P(None, 'gy', ('gx', 'gz')), may hold values from -40 to 40
- norm_gain: float32 [4, 8192], P('section', 'gx'), may hold values from 0.5 to 1.5
- q_weight: bfloat16 [4, 8192, 8192], P('section', ('gx', 'gy'), 'gz'), may hold values from -0.0625 to 0.0625
- kv_weight: bfloat16 [4, 2, 8192, 1024], P('section', None, ('gx', 'gy'), 'gz'), may hold values from -0.0625 to 0.0625
- q_bias: float32 [4, 8192], P('section', 'gz'), may hold values from -130 to 130
- kv_bias: float32 [4, 2, 1024], P('section', None, 'gz'), may hold values from -50 to 50
- out_weight: bfloat16 [4, 8192, 8192], P('section', 'gz', ('gx', 'gy')), may hold values from -0.0625 to 0.0625
Outputs:
- hidden_out: bfloat16 [4, 1, 256, 8192], P('section', None, 'gy', ('gx', 'gz'))
All inputs are finite; a program needn't handle non-finite values.
Results may differ from a plain program's by a relative error of at most 0.025.
Values may be sent and summed in bfloat16 or wider, within the bound.
No kernel may reach another device: no remote copies, remote signals or barrier semaphores. Data moves between devices by JAX's collectives and lax.ppermute only.
A program may use at most 128 MiB of HBM per device.

v0:
```python
import jax
import jax.numpy as jnp
from jax import lax
from jax.sharding import PartitionSpec as P

D = 8192
HD = 128
ROPE_BASE = 1000000.0
EPSILON = 1e-06
NEG_FILL = -1e30


def from_behind(value, axis, steps):
    count = lax.axis_size(axis)
    initial, last = (max(0, -steps), min(count, count - steps))
    return lax.ppermute(value, axis, [(source, source + steps) for source in range(initial, last)])


def rotary(values, positions):
    half_width = values.shape[-1] // 2
    frequency = ROPE_BASE ** (-jnp.arange(half_width, dtype=jnp.float32) * 2.0 / values.shape[-1])
    angles = positions.astype(jnp.float32)[:, None] * frequency[None, :]
    cosine = jnp.cos(angles)[:, None, :]
    sine_part = jnp.sin(angles)[:, None, :]
    lower_half = values[..., :half_width]
    upper_half = values[..., half_width:]
    return jnp.concatenate(
        [
            lower_half * cosine - upper_half * sine_part,
            upper_half * cosine + lower_half * sine_part,
        ],
        axis=-1,
    )


def body(micro_inputs, norm_gain, q_weight, kv_weight, q_bias, kv_bias, out_weight):
    section_count = lax.axis_size("section")
    size_gx = lax.axis_size("gx")
    micro_count = micro_inputs.shape[0]
    local_rows = micro_inputs.shape[1]
    index_gx = lax.axis_index("gx")
    index_gy = lax.axis_index("gy")
    index_section = lax.axis_index("section")
    query_weight = q_weight[0]
    pair_weight = jnp.concatenate([kv_weight[0, 0], kv_weight[0, 1]], axis=1)
    mixing_weight = out_weight[0]
    slab_rows = q_weight.shape[1]
    q_cols = query_weight.shape[1]
    kv_cols = pair_weight.shape[1] // 2
    gain_row = norm_gain[0]
    q_heads = q_cols // HD
    kv_heads = kv_cols // HD
    group_size = q_heads // kv_heads
    own_cols = q_cols // size_gx
    own_heads = own_cols // HD
    if own_heads > group_size:
        used_heads = own_heads // group_size
        local_group = group_size
    else:
        used_heads = 1
        local_group = own_heads
    used_start = index_gx * own_heads // group_size
    score_scale = HD ** (-0.5)
    row_pos = index_gy * local_rows + jnp.arange(local_rows)
    own_bias = lax.dynamic_slice_in_dim(q_bias[0], index_gx * own_cols, own_cols, 0)

    def mix_cols(piece):
        return jnp.dot(piece, mixing_weight, preferred_element_type=jnp.float32)

    def attention_layer(wide_block):
        widened = wide_block.astype(jnp.float32)
        squares = lax.psum(jnp.sum(widened * widened, axis=1), "gx")
        normed = (widened * lax.rsqrt(squares / D + EPSILON)[:, None] * gain_row[None, :]).astype(
            jnp.bfloat16
        )
        all_tokens = lax.all_gather(normed, "gy", axis=0, tiled=True)
        own_slab = lax.dynamic_slice_in_dim(all_tokens, index_gy * slab_rows, slab_rows, 1)
        query_part = jnp.dot(own_slab, query_weight, preferred_element_type=jnp.float32)
        pair_part = jnp.dot(own_slab, pair_weight, preferred_element_type=jnp.float32)
        query_rows, pair_local = (
            lax.psum_scatter(
                query_part.astype(jnp.bfloat16), "gy", scatter_dimension=0, tiled=True
            ).astype(jnp.float32),
            lax.psum_scatter(
                pair_part.astype(jnp.bfloat16), "gy", scatter_dimension=0, tiled=True
            ).astype(jnp.float32),
        )
        queries = (
            lax.psum_scatter(
                query_rows.astype(jnp.bfloat16), "gx", scatter_dimension=1, tiled=True
            ).astype(jnp.float32)
            + own_bias[None, :]
        )
        pair_terms = lax.psum(pair_local.astype(jnp.bfloat16), "gx").astype(jnp.float32)
        key_rows = pair_terms[:, :kv_cols] + kv_bias[0, 0][None, :]
        value_rows = (pair_terms[:, kv_cols:] + kv_bias[0, 1][None, :]).astype(jnp.bfloat16)
        queries = rotary(queries.reshape(local_rows, own_heads, HD), row_pos).astype(jnp.bfloat16)
        queries = queries.reshape(local_rows, used_heads, local_group, HD)
        key_rows = rotary(key_rows.reshape(local_rows, kv_heads, HD), row_pos).astype(jnp.bfloat16)
        key_used = lax.dynamic_slice_in_dim(key_rows, used_start, used_heads, 1).reshape(
            local_rows, used_heads * HD
        )
        value_used = lax.dynamic_slice_in_dim(
            value_rows.reshape(local_rows, kv_heads, HD), used_start, used_heads, 1
        ).reshape(local_rows, used_heads * HD)
        running_max = jnp.full((used_heads, local_group, local_rows), NEG_FILL, jnp.float32)
        key_piece = lax.all_gather(key_used, "gy", axis=0, tiled=True)
        value_piece = lax.all_gather(value_used, "gy", axis=0, tiled=True)
        key_count = key_piece.shape[0]
        key_pos = jnp.arange(key_count)
        scores = (
            jnp.einsum(
                "qhgd,khd->hgqk",
                queries,
                key_piece.reshape(key_count, used_heads, HD),
                preferred_element_type=jnp.float32,
            )
            * score_scale
        )
        allowed = key_pos[None, :] <= row_pos[:, None]
        scores = jnp.where(allowed, scores, NEG_FILL)
        new_max = jnp.maximum(running_max, jnp.max(scores, axis=-1))
        weights = jnp.where(allowed, jnp.exp(scores - new_max[..., None]), 0.0)
        running_sum = jnp.sum(weights, axis=-1)
        update = jnp.einsum(
            "hgqk,khd->qhgd",
            weights.astype(jnp.bfloat16),
            value_piece.reshape(key_count, used_heads, HD),
            preferred_element_type=jnp.float32,
        )
        weighted = update
        running_max, running_sum, weighted = (new_max, running_sum, weighted)
        attended = (
            (weighted / jnp.transpose(running_sum, (2, 0, 1))[..., None])
            .astype(jnp.bfloat16)
            .reshape(local_rows, own_cols)
        )
        every_token = lax.all_gather(attended, "gy", axis=0, tiled=True)
        column_sums = mix_cols(lax.all_gather(every_token, "gx", axis=1, tiled=True))
        return lax.all_to_all(
            column_sums.astype(jnp.bfloat16), "gy", split_axis=0, concat_axis=1, tiled=True
        ).astype(column_sums.dtype)

    def record(stored, tick_index, result):
        micro_index = tick_index - index_section
        is_valid = (micro_index >= 0) & (micro_index < micro_count)
        clipped = jnp.clip(micro_index, 0, micro_count - 1)
        previous = lax.dynamic_index_in_dim(stored, clipped, 0, keepdims=False)
        return lax.dynamic_update_index_in_dim(
            stored, jnp.where(is_valid, result, previous), clipped, 0
        )

    tick_count = micro_count + section_count - 1
    stored_start = jnp.zeros(micro_inputs.shape, jnp.bfloat16)

    def advance(tick_index, state):
        carried, stored = state
        fresh = lax.dynamic_index_in_dim(
            micro_inputs, jnp.clip(tick_index, 0, micro_count - 1), 0, keepdims=False
        )
        current = jnp.where(index_section == 0, fresh, carried)
        wide_block = lax.all_gather(current, "gz", axis=1, tiled=True)
        summed = lax.psum_scatter(
            attention_layer(wide_block).astype(jnp.bfloat16), "gz", scatter_dimension=1, tiled=True
        ).astype(jnp.float32)
        result = (current.astype(jnp.float32) + summed).astype(jnp.bfloat16)
        stored = record(stored, tick_index, result)
        return (from_behind(result, "section", 1), stored)

    carry_start = jnp.zeros(micro_inputs.shape[1:], jnp.bfloat16)
    final_state = lax.fori_loop(0, tick_count, advance, (carry_start, stored_start))
    return final_state[1][None]


def solution(mesh):
    return jax.shard_map(
        body,
        mesh=mesh,
        in_specs=(
            P(None, "gy", ("gx", "gz")),
            P("section", "gx"),
            P("section", ("gx", "gy"), "gz"),
            P("section", None, ("gx", "gy"), "gz"),
            P("section", "gz"),
            P("section", None, "gz"),
            P("section", "gz", ("gx", "gy")),
        ),
        out_specs=P("section", None, "gy", ("gx", "gz")),
        check_vma=False,
    )
```

profile of v0, /device:TPU:0, one launch (start us, length us, event | category | flops | bytes accessed | tf_op | source)
XLA Modules:
  0.0 1107.2 jit_solution(5537659410085549743)
XLA Ops:
  12.5 1087.3 %while.19 = (s32[]{:T(128)}, bf16[128,2048]{1,0:T(8,128)(2,1)S(1)}, bf16[1,128,2048]{2,1,0:T(8,128)(2,1)S(1)}, pred[]{:T(512)}, bf16[1,128,2048]{2,1,0:T(8,128)(...) while((s32[]{:T(128)}, bf16[128,2048]{1,0:T(8,128)(2,1)S(1)}, ...), condition=%wide.region_10.11_spmd.clone.clone, body=%wide.region_0.10_spmd.clone.clone.sunk | while | flops 9950043136 | bytes 130518144 | solution.py:171
  13.5 13.2 %all-gather.5.cloned.1.call-done = bf16[128,4096]{1,0:T(8,128)(2,1)} async-done(((bf16[128,2048]{1,0:T(8,128)(2,1)}), bf16[128,4096]{1,0:T(8,128)(2,1)}) %all-gather.5.cloned.1.call-update) | async-done | bytes 1048592 | tf_op jit(solution)/shard_map/while/body/eval_jaxpr/all_gather | solution.py:162
  35.8 34.4 %all-gather.7.cloned.1.call-done = bf16[256,4096]{1,0:T(8,128)(2,1)} async-done(((bf16[128,4096]{1,0:T(8,128)(2,1)}), bf16[256,4096]{1,0:T(8,128)(2,1)}) %all-gather.7.cloned.1.call-update) | async-done | bytes 2097168 | tf_op jit(solution)/shard_map/while/body/eval_jaxpr/all_gather | solution.py:76
  74.8 12.0 %convolution_convert_fusion.7 = bf16[256,4096]{1,0:T(8,128)(2,1)} fusion(bf16[2048,4096]{1,0:T(8,128)(2,1)} %get-tuple-element.638, bf16[256,4096]{1,0:T(8,128)(2,1)} %all-gather.7.cloned.1.call-done, s32[]{:T(128)} %get-tuple-element.634), kind=kOutput, calls=%fused_computation.2.clone.1 | convolution fusion | flops 4296015872 | bytes 19923456 | tf_op jit(solution)/shard_map/while/body/eval_jaxpr/dot_general | solution.py:78
  89.7 34.0 %reduce-scatter.7.cloned.1.call-done = bf16[128,4096]{1,0:T(8,128)(2,1)} async-done(((bf16[256,4096]{1,0:T(8,128)(2,1)}), bf16[128,4096]{1,0:T(8,128)(2,1)}) %reduce-scatter.7.cloned.1.call-update) | async-done | bytes 1048592 | tf_op jit(solution)/shard_map/while/body/eval_jaxpr/reduce_scatter | solution.py:81
  124.1 25.0 %all-reduce.2.cloned.1.call-done = bf16[128,1024]{1,0:T(8,128)(2,1)} async-done(((bf16[128,1024]{1,0:T(8,128)(2,1)}), bf16[128,1024]{1,0:T(8,128)(2,1)}) %all-reduce.2.cloned.1.call-update) | async-done | bytes 262160 | tf_op jit(solution)/shard_map/while/body/eval_jaxpr/psum | solution.py:94
  161.0 10.6 reduce-scatter.9.cloned.1.call-done
  176.5 21.4 %all-gather.9.cloned.1.call-done = bf16[256,2048]{0,1:T(8,128)(2,1)} async-done(((bf16[128,2048]{0,1:T(8,128)(2,1)}), bf16[256,2048]{0,1:T(8,128)(2,1)}) %all-gather.9.cloned.1.call-update) | async-done | bytes 1048592 | tf_op jit(solution)/shard_map/while/body/eval_jaxpr/all_gather | solution.py:138
  197.9 34.6 %all-gather.11.cloned.1.call-done = bf16[256,4096]{0,1:T(8,128)(2,1)} async-done(((bf16[256,2048]{0,1:T(8,128)(2,1)}), bf16[256,4096]{0,1:T(8,128)(2,1)}) %all-gather.11.cloned.1.call-update) | async-done | bytes 2097168 | tf_op jit(solution)/shard_map/while/body/eval_jaxpr/all_gather | solution.py:139
  232.5 10.9 convolution_convert_fusion.8
  243.5 16.2 %all_to_all.48 = bf16[2,128,2048]{2,1,0:T(8,128)(2,1)S(1)} all-to-all(bf16[2,128,2048]{2,1,0:T(8,128)(2,1)S(1)} %bitcast.132), channel_id=1, replica_groups=mesh['section'=4,'gx'=2,'gy'=2,'gz'=2] {'gy'}, dimensions={0} | all-to-all | bytes 2097152 | tf_op jit(solution)/shard_map/while/body/eval_jaxpr/all_to_all | solution.py:140
  273.4 11.6 %collective-permute-done = bf16[128,2048]{1,0:T(8,128)(2,1)S(1)} collective-permute-done((bf16[128,2048]{1,0:T(8,128)(2,1)S(1)}, bf16[128,2048]{1,0:T(8,128)(2,1)S(1)}, u32[]{:S(2)}, u32[]{:S(2)}) %collective-permute-start) | collective-permute-done | bytes 524320 | tf_op jit(solution)/shard_map/while/body/eval_jaxpr/ppermute | solution.py:16
  285.9 12.1 %all-gather.5.cloned.1.call-done = bf16[128,4096]{1,0:T(8,128)(2,1)} async-done(((bf16[128,2048]{1,0:T(8,128)(2,1)}), bf16[128,4096]{1,0:T(8,128)(2,1)}) %all-gather.5.cloned.1.call-update) | async-done | bytes 1048592 | tf_op jit(solution)/shard_map/while/body/eval_jaxpr/all_gather | solution.py:162
  307.0 34.4 %all-gather.7.cloned.1.call-done = bf16[256,4096]{1,0:T(8,128)(2,1)} async-done(((bf16[128,4096]{1,0:T(8,128)(2,1)}), bf16[256,4096]{1,0:T(8,128)(2,1)}) %all-gather.7.cloned.1.call-update) | async-done | bytes 2097168 | tf_op jit(solution)/shard_map/while/body/eval_jaxpr/all_gather | solution.py:76
  346.1 12.0 %convolution_convert_fusion.7 = bf16[256,4096]{1,0:T(8,128)(2,1)} fusion(bf16[2048,4096]{1,0:T(8,128)(2,1)} %get-tuple-element.638, bf16[256,4096]{1,0:T(8,128)(2,1)} %all-gather.7.cloned.1.call-done, s32[]{:T(128)} %get-tuple-element.634), kind=kOutput, calls=%fused_computation.2.clone.1 | convolution fusion | flops 4296015872 | bytes 19923456 | tf_op jit(solution)/shard_map/while/body/eval_jaxpr/dot_general | solution.py:78
  360.9 34.1 %reduce-scatter.7.cloned.1.call-done = bf16[128,4096]{1,0:T(8,128)(2,1)} async-done(((bf16[256,4096]{1,0:T(8,128)(2,1)}), bf16[128,4096]{1,0:T(8,128)(2,1)}) %reduce-scatter.7.cloned.1.call-update) | async-done | bytes 1048592 | tf_op jit(solution)/shard_map/while/body/eval_jaxpr/reduce_scatter | solution.py:81
  395.5 25.0 %all-reduce.2.cloned.1.call-done = bf16[128,1024]{1,0:T(8,128)(2,1)} async-done(((bf16[128,1024]{1,0:T(8,128)(2,1)}), bf16[128,1024]{1,0:T(8,128)(2,1)}) %all-reduce.2.cloned.1.call-update) | async-done | bytes 262160 | tf_op jit(solution)/shard_map/while/body/eval_jaxpr/psum | solution.py:94
  432.4 10.6 reduce-scatter.9.cloned.1.call-done
  447.9 21.4 %all-gather.9.cloned.1.call-done = bf16[256,2048]{0,1:T(8,128)(2,1)} async-done(((bf16[128,2048]{0,1:T(8,128)(2,1)}), bf16[256,2048]{0,1:T(8,128)(2,1)}) %all-gather.9.cloned.1.call-update) | async-done | bytes 1048592 | tf_op jit(solution)/shard_map/while/body/eval_jaxpr/all_gather | solution.py:138
  469.4 34.4 %all-gather.11.cloned.1.call-done = bf16[256,4096]{0,1:T(8,128)(2,1)} async-done(((bf16[256,2048]{0,1:T(8,128)(2,1)}), bf16[256,4096]{0,1:T(8,128)(2,1)}) %all-gather.11.cloned.1.call-update) | async-done | bytes 2097168 | tf_op jit(solution)/shard_map/while/body/eval_jaxpr/all_gather | solution.py:139
  503.8 10.9 convolution_convert_fusion.8
  514.7 16.2 %all_to_all.48 = bf16[2,128,2048]{2,1,0:T(8,128)(2,1)S(1)} all-to-all(bf16[2,128,2048]{2,1,0:T(8,128)(2,1)S(1)} %bitcast.132), channel_id=1, replica_groups=mesh['section'=4,'gx'=2,'gy'=2,'gz'=2] {'gy'}, dimensions={0} | all-to-all | bytes 2097152 | tf_op jit(solution)/shard_map/while/body/eval_jaxpr/all_to_all | solution.py:140
  532.0 7.6 reduce-scatter.11.cloned.1.call-done
  544.6 11.6 %collective-permute-done = bf16[128,2048]{1,0:T(8,128)(2,1)S(1)} collective-permute-done((bf16[128,2048]{1,0:T(8,128)(2,1)S(1)}, bf16[128,2048]{1,0:T(8,128)(2,1)S(1)}, u32[]{:S(2)}, u32[]{:S(2)}) %collective-permute-start) | collective-permute-done | bytes 524320 | tf_op jit(solution)/shard_map/while/body/eval_jaxpr/ppermute | solution.py:16
  557.1 12.4 %all-gather.5.cloned.1.call-done = bf16[128,4096]{1,0:T(8,128)(2,1)} async-done(((bf16[128,2048]{1,0:T(8,128)(2,1)}), bf16[128,4096]{1,0:T(8,128)(2,1)}) %all-gather.5.cloned.1.call-update) | async-done | bytes 1048592 | tf_op jit(solution)/shard_map/while/body/eval_jaxpr/all_gather | solution.py:162
  578.6 34.4 %all-gather.7.cloned.1.call-done = bf16[256,4096]{1,0:T(8,128)(2,1)} async-done(((bf16[128,4096]{1,0:T(8,128)(2,1)}), bf16[256,4096]{1,0:T(8,128)(2,1)}) %all-gather.7.cloned.1.call-update) | async-done | bytes 2097168 | tf_op jit(solution)/shard_map/while/body/eval_jaxpr/all_gather | solution.py:76
  617.7 12.0 %convolution_convert_fusion.7 = bf16[256,4096]{1,0:T(8,128)(2,1)} fusion(bf16[2048,4096]{1,0:T(8,128)(2,1)} %get-tuple-element.638, bf16[256,4096]{1,0:T(8,128)(2,1)} %all-gather.7.cloned.1.call-done, s32[]{:T(128)} %get-tuple-element.634), kind=kOutput, calls=%fused_computation.2.clone.1 | convolution fusion | flops 4296015872 | bytes 19923456 | tf_op jit(solution)/shard_map/while/body/eval_jaxpr/dot_general | solution.py:78
  632.5 34.1 %reduce-scatter.7.cloned.1.call-done = bf16[128,4096]{1,0:T(8,128)(2,1)} async-done(((bf16[256,4096]{1,0:T(8,128)(2,1)}), bf16[128,4096]{1,0:T(8,128)(2,1)}) %reduce-scatter.7.cloned.1.call-update) | async-done | bytes 1048592 | tf_op jit(solution)/shard_map/while/body/eval_jaxpr/reduce_scatter | solution.py:81
  667.1 25.1 %all-reduce.2.cloned.1.call-done = bf16[128,1024]{1,0:T(8,128)(2,1)} async-done(((bf16[128,1024]{1,0:T(8,128)(2,1)}), bf16[128,1024]{1,0:T(8,128)(2,1)}) %all-reduce.2.cloned.1.call-update) | async-done | bytes 262160 | tf_op jit(solution)/shard_map/while/body/eval_jaxpr/psum | solution.py:94
  704.1 10.6 reduce-scatter.9.cloned.1.call-done
  719.7 21.4 %all-gather.9.cloned.1.call-done = bf16[256,2048]{0,1:T(8,128)(2,1)} async-done(((bf16[128,2048]{0,1:T(8,128)(2,1)}), bf16[256,2048]{0,1:T(8,128)(2,1)}) %all-gather.9.cloned.1.call-update) | async-done | bytes 1048592 | tf_op jit(solution)/shard_map/while/body/eval_jaxpr/all_gather | solution.py:138
  741.1 34.4 %all-gather.11.cloned.1.call-done = bf16[256,4096]{0,1:T(8,128)(2,1)} async-done(((bf16[256,2048]{0,1:T(8,128)(2,1)}), bf16[256,4096]{0,1:T(8,128)(2,1)}) %all-gather.11.cloned.1.call-update) | async-done | bytes 2097168 | tf_op jit(solution)/shard_map/while/body/eval_jaxpr/all_gather | solution.py:139
  775.5 10.9 convolution_convert_fusion.8
  786.4 16.2 %all_to_all.48 = bf16[2,128,2048]{2,1,0:T(8,128)(2,1)S(1)} all-to-all(bf16[2,128,2048]{2,1,0:T(8,128)(2,1)S(1)} %bitcast.132), channel_id=1, replica_groups=mesh['section'=4,'gx'=2,'gy'=2,'gz'=2] {'gy'}, dimensions={0} | all-to-all | bytes 2097152 | tf_op jit(solution)/shard_map/while/body/eval_jaxpr/all_to_all | solution.py:140
  803.7 7.6 reduce-scatter.11.cloned.1.call-done
  816.4 11.6 %collective-permute-done = bf16[128,2048]{1,0:T(8,128)(2,1)S(1)} collective-permute-done((bf16[128,2048]{1,0:T(8,128)(2,1)S(1)}, bf16[128,2048]{1,0:T(8,128)(2,1)S(1)}, u32[]{:S(2)}, u32[]{:S(2)}) %collective-permute-start) | collective-permute-done | bytes 524320 | tf_op jit(solution)/shard_map/while/body/eval_jaxpr/ppermute | solution.py:16
  828.9 12.4 %all-gather.5.cloned.1.call-done = bf16[128,4096]{1,0:T(8,128)(2,1)} async-done(((bf16[128,2048]{1,0:T(8,128)(2,1)}), bf16[128,4096]{1,0:T(8,128)(2,1)}) %all-gather.5.cloned.1.call-update) | async-done | bytes 1048592 | tf_op jit(solution)/shard_map/while/body/eval_jaxpr/all_gather | solution.py:162
  850.4 34.4 %all-gather.7.cloned.1.call-done = bf16[256,4096]{1,0:T(8,128)(2,1)} async-done(((bf16[128,4096]{1,0:T(8,128)(2,1)}), bf16[256,4096]{1,0:T(8,128)(2,1)}) %all-gather.7.cloned.1.call-update) | async-done | bytes 2097168 | tf_op jit(solution)/shard_map/while/body/eval_jaxpr/all_gather | solution.py:76
  889.4 12.0 %convolution_convert_fusion.7 = bf16[256,4096]{1,0:T(8,128)(2,1)} fusion(bf16[2048,4096]{1,0:T(8,128)(2,1)} %get-tuple-element.638, bf16[256,4096]{1,0:T(8,128)(2,1)} %all-gather.7.cloned.1.call-done, s32[]{:T(128)} %get-tuple-element.634), kind=kOutput, calls=%fused_computation.2.clone.1 | convolution fusion | flops 4296015872 | bytes 19923456 | tf_op jit(solution)/shard_map/while/body/eval_jaxpr/dot_general | solution.py:78
  904.2 34.1 %reduce-scatter.7.cloned.1.call-done = bf16[128,4096]{1,0:T(8,128)(2,1)} async-done(((bf16[256,4096]{1,0:T(8,128)(2,1)}), bf16[128,4096]{1,0:T(8,128)(2,1)}) %reduce-scatter.7.cloned.1.call-update) | async-done | bytes 1048592 | tf_op jit(solution)/shard_map/while/body/eval_jaxpr/reduce_scatter | solution.py:81
  938.8 25.1 %all-reduce.2.cloned.1.call-done = bf16[128,1024]{1,0:T(8,128)(2,1)} async-done(((bf16[128,1024]{1,0:T(8,128)(2,1)}), bf16[128,1024]{1,0:T(8,128)(2,1)}) %all-reduce.2.cloned.1.call-update) | async-done | bytes 262160 | tf_op jit(solution)/shard_map/while/body/eval_jaxpr/psum | solution.py:94
  975.9 10.6 reduce-scatter.9.cloned.1.call-done
  991.4 21.4 %all-gather.9.cloned.1.call-done = bf16[256,2048]{0,1:T(8,128)(2,1)} async-done(((bf16[128,2048]{0,1:T(8,128)(2,1)}), bf16[256,2048]{0,1:T(8,128)(2,1)}) %all-gather.9.cloned.1.call-update) | async-done | bytes 1048592 | tf_op jit(solution)/shard_map/while/body/eval_jaxpr/all_gather | solution.py:138
  1012.8 34.6 %all-gather.11.cloned.1.call-done = bf16[256,4096]{0,1:T(8,128)(2,1)} async-done(((bf16[256,2048]{0,1:T(8,128)(2,1)}), bf16[256,4096]{0,1:T(8,128)(2,1)}) %all-gather.11.cloned.1.call-update) | async-done | bytes 2097168 | tf_op jit(solution)/shard_map/while/body/eval_jaxpr/all_gather | solution.py:139
  1047.4 10.9 convolution_convert_fusion.8
  1058.3 16.2 %all_to_all.48 = bf16[2,128,2048]{2,1,0:T(8,128)(2,1)S(1)} all-to-all(bf16[2,128,2048]{2,1,0:T(8,128)(2,1)S(1)} %bitcast.132), channel_id=1, replica_groups=mesh['section'=4,'gx'=2,'gy'=2,'gz'=2] {'gy'}, dimensions={0} | all-to-all | bytes 2097152 | tf_op jit(solution)/shard_map/while/body/eval_jaxpr/all_to_all | solution.py:140
  1075.6 7.6 reduce-scatter.11.cloned.1.call-done
  1088.3 11.6 %collective-permute-done = bf16[128,2048]{1,0:T(8,128)(2,1)S(1)} collective-permute-done((bf16[128,2048]{1,0:T(8,128)(2,1)S(1)}, bf16[128,2048]{1,0:T(8,128)(2,1)S(1)}, u32[]{:S(2)}, u32[]{:S(2)}) %collective-permute-start) | collective-permute-done | bytes 524320 | tf_op jit(solution)/shard_map/while/body/eval_jaxpr/ppermute | solution.py:16
  (238 shorter events, 177.3 us)
Async XLA Ops:
  9.8 2.8 copy-start.4
  9.8 2.8 copy-start.5
  9.8 2.8 copy-start.6
  12.6 14.1 %all-gather.5.cloned.1.call-start = ((), (), s32[]{:S(2)}) async-start(), calls=%async_computation.5 | async-start | bytes 1572864 | tf_op jit(solution)/shard_map/while/body/eval_jaxpr/all_gather | solution.py:162
  13.5 56.7 %all-gather.7.cloned.1.call-start = ((), (), s32[]{:S(2)}) async-start(), calls=%async_computation.6 | async-start | bytes 3145728 | tf_op jit(solution)/shard_map/while/body/eval_jaxpr/all_gather | solution.py:76
  35.7 53.9 %reduce-scatter.5.cloned.1.call-start = ((), (), s32[]{:S(2)}) async-start(), calls=%async_computation.7 | async-start | bytes 786432 | tf_op jit(solution)/shard_map/while/body/eval_jaxpr/reduce_scatter | solution.py:84
  74.8 48.8 %reduce-scatter.7.cloned.1.call-start = ((), (), s32[]{:S(2)}) async-start(), calls=%async_computation.9 | async-start | bytes 3145728 | tf_op jit(solution)/shard_map/while/body/eval_jaxpr/reduce_scatter | solution.py:81
  86.8 62.2 %all-reduce.2.cloned.1.call-start = ((), (), s32[]{:S(2)}) async-start(), calls=%async_computation.8 | async-start | bytes 524288 | tf_op jit(solution)/shard_map/while/body/eval_jaxpr/psum | solution.py:94
  89.6 82.0 %reduce-scatter.9.cloned.1.call-start = ((), (), s32[]{:S(2)}) async-start(), calls=%async_computation.10 | async-start | bytes 1572864 | tf_op jit(solution)/shard_map/while/body/eval_jaxpr/reduce_scatter | solution.py:89
  123.7 74.2 %all-gather.9.cloned.1.call-start = ((), (), s32[]{:S(2)}) async-start(), calls=%async_computation.11 | async-start | bytes 1572864 | tf_op jit(solution)/shard_map/while/body/eval_jaxpr/all_gather | solution.py:138
  176.5 56.1 %all-gather.11.cloned.1.call-start = ((), (), s32[]{:S(2)}) async-start(), calls=%async_computation.12 | async-start | bytes 3145728 | tf_op jit(solution)/shard_map/while/body/eval_jaxpr/all_gather | solution.py:139
  197.9 70.4 %reduce-scatter.11.cloned.1.call-start = ((), (), s32[]{:S(2)}) async-start(), calls=%async_computation.13 | async-start | bytes 1572864 | tf_op jit(solution)/shard_map/while/body/eval_jaxpr/reduce_scatter | solution.py:163
  259.6 8.7 copy-start.2
  269.7 15.3 %collective-permute-start = (bf16[128,2048]{1,0:T(8,128)(2,1)S(1)}, bf16[128,2048]{1,0:T(8,128)(2,1)S(1)}, u32[]{:S(2)}, u32[]{:S(2)}) collective-permute-start(bf16[128,2048]{1,0:T(8,128)(2,1)S(1)} %get-tuple-element.592), channel_id=1, source_target_pairs={{0,8},{8,16},{16,24},{1,9},{9,17},{17,25},{2,10},{10,18},{18,26},{... | collective-permute-start | bytes 1572872 | tf_op jit(solution)/shard_map/while/body/eval_jaxpr/ppermute | solution.py:16
  285.0 13.0 %all-gather.5.cloned.1.call-start = ((), (), s32[]{:S(2)}) async-start(), calls=%async_computation.5 | async-start | bytes 1572864 | tf_op jit(solution)/shard_map/while/body/eval_jaxpr/all_gather | solution.py:162
  285.8 55.6 %all-gather.7.cloned.1.call-start = ((), (), s32[]{:S(2)}) async-start(), calls=%async_computation.6 | async-start | bytes 3145728 | tf_op jit(solution)/shard_map/while/body/eval_jaxpr/all_gather | solution.py:76
  307.0 53.9 %reduce-scatter.5.cloned.1.call-start = ((), (), s32[]{:S(2)}) async-start(), calls=%async_computation.7 | async-start | bytes 786432 | tf_op jit(solution)/shard_map/while/body/eval_jaxpr/reduce_scatter | solution.py:84
  346.1 49.0 %reduce-scatter.7.cloned.1.call-start = ((), (), s32[]{:S(2)}) async-start(), calls=%async_computation.9 | async-start | bytes 3145728 | tf_op jit(solution)/shard_map/while/body/eval_jaxpr/reduce_scatter | solution.py:81
  358.1 62.4 %all-reduce.2.cloned.1.call-start = ((), (), s32[]{:S(2)}) async-start(), calls=%async_computation.8 | async-start | bytes 524288 | tf_op jit(solution)/shard_map/while/body/eval_jaxpr/psum | solution.py:94
  360.9 82.1 %reduce-scatter.9.cloned.1.call-start = ((), (), s32[]{:S(2)}) async-start(), calls=%async_computation.10 | async-start | bytes 1572864 | tf_op jit(solution)/shard_map/while/body/eval_jaxpr/reduce_scatter | solution.py:89
  395.1 74.2 %all-gather.9.cloned.1.call-start = ((), (), s32[]{:S(2)}) async-start(), calls=%async_computation.11 | async-start | bytes 1572864 | tf_op jit(solution)/shard_map/while/body/eval_jaxpr/all_gather | solution.py:138
  447.9 55.9 %all-gather.11.cloned.1.call-start = ((), (), s32[]{:S(2)}) async-start(), calls=%async_computation.12 | async-start | bytes 3145728 | tf_op jit(solution)/shard_map/while/body/eval_jaxpr/all_gather | solution.py:139
  469.3 70.3 %reduce-scatter.11.cloned.1.call-start = ((), (), s32[]{:S(2)}) async-start(), calls=%async_computation.13 | async-start | bytes 1572864 | tf_op jit(solution)/shard_map/while/body/eval_jaxpr/reduce_scatter | solution.py:163
  530.9 8.7 copy-start.2
  540.9 15.3 %collective-permute-start = (bf16[128,2048]{1,0:T(8,128)(2,1)S(1)}, bf16[128,2048]{1,0:T(8,128)(2,1)S(1)}, u32[]{:S(2)}, u32[]{:S(2)}) collective-permute-start(bf16[128,2048]{1,0:T(8,128)(2,1)S(1)} %get-tuple-element.592), channel_id=1, source_target_pairs={{0,8},{8,16},{16,24},{1,9},{9,17},{17,25},{2,10},{10,18},{18,26},{... | collective-permute-start | bytes 1572872 | tf_op jit(solution)/shard_map/while/body/eval_jaxpr/ppermute | solution.py:16
  556.2 13.3 %all-gather.5.cloned.1.call-start = ((), (), s32[]{:S(2)}) async-start(), calls=%async_computation.5 | async-start | bytes 1572864 | tf_op jit(solution)/shard_map/while/body/eval_jaxpr/all_gather | solution.py:162
  557.1 55.9 %all-gather.7.cloned.1.call-start = ((), (), s32[]{:S(2)}) async-start(), calls=%async_computation.6 | async-start | bytes 3145728 | tf_op jit(solution)/shard_map/while/body/eval_jaxpr/all_gather | solution.py:76
  578.6 53.9 %reduce-scatter.5.cloned.1.call-start = ((), (), s32[]{:S(2)}) async-start(), calls=%async_computation.7 | async-start | bytes 786432 | tf_op jit(solution)/shard_map/while/body/eval_jaxpr/reduce_scatter | solution.py:84
  617.6 49.0 %reduce-scatter.7.cloned.1.call-start = ((), (), s32[]{:S(2)}) async-start(), calls=%async_computation.9 | async-start | bytes 3145728 | tf_op jit(solution)/shard_map/while/body/eval_jaxpr/reduce_scatter | solution.py:81
  629.7 62.5 %all-reduce.2.cloned.1.call-start = ((), (), s32[]{:S(2)}) async-start(), calls=%async_computation.8 | async-start | bytes 524288 | tf_op jit(solution)/shard_map/while/body/eval_jaxpr/psum | solution.py:94
  632.5 82.3 %reduce-scatter.9.cloned.1.call-start = ((), (), s32[]{:S(2)}) async-start(), calls=%async_computation.10 | async-start | bytes 1572864 | tf_op jit(solution)/shard_map/while/body/eval_jaxpr/reduce_scatter | solution.py:89
  666.6 74.4 %all-gather.9.cloned.1.call-start = ((), (), s32[]{:S(2)}) async-start(), calls=%async_computation.11 | async-start | bytes 1572864 | tf_op jit(solution)/shard_map/while/body/eval_jaxpr/all_gather | solution.py:138
  719.6 55.9 %all-gather.11.cloned.1.call-start = ((), (), s32[]{:S(2)}) async-start(), calls=%async_computation.12 | async-start | bytes 3145728 | tf_op jit(solution)/shard_map/while/body/eval_jaxpr/all_gather | solution.py:139
  741.0 70.3 %reduce-scatter.11.cloned.1.call-start = ((), (), s32[]{:S(2)}) async-start(), calls=%async_computation.13 | async-start | bytes 1572864 | tf_op jit(solution)/shard_map/while/body/eval_jaxpr/reduce_scatter | solution.py:163
  802.6 8.7 copy-start.2
  812.7 15.3 %collective-permute-start = (bf16[128,2048]{1,0:T(8,128)(2,1)S(1)}, bf16[128,2048]{1,0:T(8,128)(2,1)S(1)}, u32[]{:S(2)}, u32[]{:S(2)}) collective-permute-start(bf16[128,2048]{1,0:T(8,128)(2,1)S(1)} %get-tuple-element.592), channel_id=1, source_target_pairs={{0,8},{8,16},{16,24},{1,9},{9,17},{17,25},{2,10},{10,18},{18,26},{... | collective-permute-start | bytes 1572872 | tf_op jit(solution)/shard_map/while/body/eval_jaxpr/ppermute | solution.py:16
  827.9 13.3 %all-gather.5.cloned.1.call-start = ((), (), s32[]{:S(2)}) async-start(), calls=%async_computation.5 | async-start | bytes 1572864 | tf_op jit(solution)/shard_map/while/body/eval_jaxpr/all_gather | solution.py:162
  828.8 55.9 %all-gather.7.cloned.1.call-start = ((), (), s32[]{:S(2)}) async-start(), calls=%async_computation.6 | async-start | bytes 3145728 | tf_op jit(solution)/shard_map/while/body/eval_jaxpr/all_gather | solution.py:76
  850.3 53.9 %reduce-scatter.5.cloned.1.call-start = ((), (), s32[]{:S(2)}) async-start(), calls=%async_computation.7 | async-start | bytes 786432 | tf_op jit(solution)/shard_map/while/body/eval_jaxpr/reduce_scatter | solution.py:84
  889.4 49.0 %reduce-scatter.7.cloned.1.call-start = ((), (), s32[]{:S(2)}) async-start(), calls=%async_computation.9 | async-start | bytes 3145728 | tf_op jit(solution)/shard_map/while/body/eval_jaxpr/reduce_scatter | solution.py:81
  901.4 62.5 %all-reduce.2.cloned.1.call-start = ((), (), s32[]{:S(2)}) async-start(), calls=%async_computation.8 | async-start | bytes 524288 | tf_op jit(solution)/shard_map/while/body/eval_jaxpr/psum | solution.py:94
  904.2 82.3 %reduce-scatter.9.cloned.1.call-start = ((), (), s32[]{:S(2)}) async-start(), calls=%async_computation.10 | async-start | bytes 1572864 | tf_op jit(solution)/shard_map/while/body/eval_jaxpr/reduce_scatter | solution.py:89
  938.4 74.4 %all-gather.9.cloned.1.call-start = ((), (), s32[]{:S(2)}) async-start(), calls=%async_computation.11 | async-start | bytes 1572864 | tf_op jit(solution)/shard_map/while/body/eval_jaxpr/all_gather | solution.py:138
  991.4 56.1 %all-gather.11.cloned.1.call-start = ((), (), s32[]{:S(2)}) async-start(), calls=%async_computation.12 | async-start | bytes 3145728 | tf_op jit(solution)/shard_map/while/body/eval_jaxpr/all_gather | solution.py:139
  1012.8 70.4 %reduce-scatter.11.cloned.1.call-start = ((), (), s32[]{:S(2)}) async-start(), calls=%async_computation.13 | async-start | bytes 1572864 | tf_op jit(solution)/shard_map/while/body/eval_jaxpr/reduce_scatter | solution.py:163
  1074.5 8.7 copy-start.2
  1084.6 15.3 %collective-permute-start = (bf16[128,2048]{1,0:T(8,128)(2,1)S(1)}, bf16[128,2048]{1,0:T(8,128)(2,1)S(1)}, u32[]{:S(2)}, u32[]{:S(2)}) collective-permute-start(bf16[128,2048]{1,0:T(8,128)(2,1)S(1)} %get-tuple-element.592), channel_id=1, source_target_pairs={{0,8},{8,16},{16,24},{1,9},{9,17},{17,25},{2,10},{10,18},{18,26},{... | collective-permute-start | bytes 1572872 | tf_op jit(solution)/shard_map/while/body/eval_jaxpr/ppermute | solution.py:16
  1099.8 0.8 copy-start.1
  (2 other events, 1.5 us)
Sparse Core Ops, SparseCore 0:
  14.9 11.7 all-gather.4
  35.8 34.2 all-gather.6
  74.9 14.6 reduce-scatter.4
  91.7 31.8 reduce-scatter.6
  125.7 23.2 all-reduce.1
  151.2 20.3 reduce-scatter.8
  176.6 21.2 all-gather.8
  199.4 33.0 all-gather.10
  260.8 7.4 reduce-scatter.10
  287.0 10.9 all-gather.4
  307.1 34.2 all-gather.6
  346.2 14.6 reduce-scatter.4
  363.1 31.8 reduce-scatter.6
  397.2 23.2 all-reduce.1
  422.6 20.3 reduce-scatter.8
  448.0 21.2 all-gather.8
  470.7 33.0 all-gather.10
  532.1 7.4 reduce-scatter.10
  558.6 10.9 all-gather.4
  578.7 34.2 all-gather.6
  617.7 14.6 reduce-scatter.4
  634.7 31.8 reduce-scatter.6
  668.9 23.2 all-reduce.1
  694.3 20.3 reduce-scatter.8
  719.7 21.2 all-gather.8
  742.4 33.0 all-gather.10
  803.8 7.4 reduce-scatter.10
  830.3 10.9 all-gather.4
  850.4 34.2 all-gather.6
  889.5 14.6 reduce-scatter.4
  906.4 31.8 reduce-scatter.6
  940.6 23.2 all-reduce.1
  966.1 20.3 reduce-scatter.8
  991.5 21.2 all-gather.8
  1014.3 33.0 all-gather.10
  1075.7 7.4 reduce-scatter.10
where the time goes:
time: 1110 us
  waiting for transfers between devices  778 us (70%)
  blocking collectives  124 us (11%)
  matrix products  118 us (11%)
  other arithmetic  44.3 us (4%)
  starting transfers between devices  16.1 us (1%)
  between operations  13.1 us (1%)
  local copies, waits for them, and re-layouts  11.5 us (1%)
    all_gather x4, waiting for transfers between devices, attention_layer(): lax.all_gather(every_token, 'gx', axis=1, tiled=True)  138 us
    all_gather x4, waiting for transfers between devices, attention_layer(): all_tokens = lax.all_gather(normed, 'gy', axis=0, tiled=True)  138 us
    reduce_scatter x4, waiting for transfers between devices, attention_layer(): lax.psum_scatter(query_part.astype(jnp.bfloat16), 'gy', scatter_dimension...  136 us
    psum x4, waiting for transfers between devices, attention_layer(): lax.psum(pair_local.astype(jnp.bfloat16), 'gx').astype(jnp.float32)  100 us
    all_gather x4, waiting for transfers between devices, attention_layer(): every_token = lax.all_gather(attended, 'gy', axis=0, tiled=True)  85.4 us
    all_to_all x4, blocking collectives, attention_layer(): lax.all_to_all(column_sums.astype(jnp.bfloat16), 'gy', split_axis=0, conc...  64.7 us
    all_gather x4, waiting for transfers between devices, advance(): wide_block = lax.all_gather(current, 'gz', axis=1, tiled=True)  50.1 us
    dot_general x4, matrix products, attention_layer(): jnp.dot(own_slab, query_weight, preferred_element_type=jnp.float32)  47.9 us
  transfers between devices with their start and end apart: 40, of which 40 were waited for; matrix products, arithmetic and copies ran while one was open for 5% of the time, Pallas kernels for 0%

commit v1 on v0

--- a/solution.py
+++ b/solution.py
@@ -136,7 +136,7 @@
             .reshape(local_rows, own_cols)
         )
         every_token = lax.all_gather(attended, "gy", axis=0, tiled=True)
-        column_sums = mix_cols(lax.all_gather(every_token, "gx", axis=1, tiled=True))
+        column_sums = mix_cols(jnp.concatenate(lax.all_gather(every_token, "gx"), axis=1))
         return lax.all_to_all(
             column_sums.astype(jnp.bfloat16), "gy", split_axis=0, concat_axis=1, tiled=True
         ).astype(column_sums.dtype)

time: 1110 us -> 1110 us (level)
  local copies, waits for them, and re-layouts: 11.5 us -> 27 us
  matrix products: 118 us -> 103 us
    reshape x0 -> x8, local copies, waits for them, and re-layouts: none -> 15.4 us  [the longest x4 11.4 us: attention_layer(): jnp.concatenate(lax.all_gather(every_token, 'gx'), axis=1)]
where the time goes in v1:
time: 1110 us
  waiting for transfers between devices  776 us (70%)
  blocking collectives  124 us (11%)
  matrix products  103 us (9%)
  other arithmetic  48.5 us (4%)
  local copies, waits for them, and re-layouts  27 us (2%)
  starting transfers between devices  16.1 us (1%)
  between operations  13.1 us (1%)
    all_gather x4, waiting for transfers between devices, attention_layer(): lax.all_gather(every_token, 'gx')  138 us
    all_gather x4, waiting for transfers between devices, attention_layer(): all_tokens = lax.all_gather(normed, 'gy', axis=0, tiled=True)  138 us
    reduce_scatter x4, waiting for transfers between devices, attention_layer(): lax.psum_scatter(query_part.astype(jnp.bfloat16), 'gy', scatter_dimension...  136 us
    psum x4, waiting for transfers between devices, attention_layer(): lax.psum(pair_local.astype(jnp.bfloat16), 'gx').astype(jnp.float32)  100 us
    all_gather x4, waiting for transfers between devices, attention_layer(): every_token = lax.all_gather(attended, 'gy', axis=0, tiled=True)  85.6 us
    all_to_all x4, blocking collectives, attention_layer(): lax.all_to_all(column_sums.astype(jnp.bfloat16), 'gy', split_axis=0, conc...  64.7 us
    ppermute x4, waiting for transfers between devices, from_behind(): lax.ppermute(value, axis, [(source, source + steps) for source in range(i...  46.3 us
    dot_general x4, matrix products, attention_layer(): jnp.dot(own_slab, query_weight, preferred_element_type=jnp.float32)  46 us
  transfers between devices with their start and end apart: 40, of which 40 were waited for; matrix products, arithmetic and copies ran while one was open for 5% of the time, Pallas kernels for 0%

profile of v1, /device:TPU:0, one launch (start us, length us, event | category | flops | bytes accessed | tf_op | source)
XLA Modules:
  0.0 1109.5 jit_solution(17893532414025848726)
XLA Ops:
  12.5 1089.6 %while.19 = (s32[]{:T(128)}, bf16[128,2048]{1,0:T(8,128)(2,1)S(1)}, bf16[1,128,2048]{2,1,0:T(8,128)(2,1)S(1)}, pred[]{:T(512)}, bf16[1,128,2048]{2,1,0:T(8,128)(...) while((s32[]{:T(128)}, bf16[128,2048]{1,0:T(8,128)(2,1)S(1)}, ...), condition=%wide.region_10.11_spmd.clone.clone, body=%wide.region_0.10_spmd.clone.clone.sunk | while | flops 9950043136 | bytes 144149136 | solution.py:171
  14.6 12.1 %all-gather.10.cloned.1.call-done = bf16[128,4096]{1,0:T(8,128)(2,1)} async-done(((bf16[128,2048]{1,0:T(8,128)(2,1)}), bf16[128,4096]{1,0:T(8,128)(2,1)}) %all-gather.10.cloned.1.call-update) | async-done | bytes 1048592 | tf_op jit(solution)/shard_map/while/body/eval_jaxpr/all_gather | solution.py:162
  35.8 34.4 %all-gather.12.cloned.1.call-done = bf16[256,4096]{1,0:T(8,128)(2,1)} async-done(((bf16[128,4096]{1,0:T(8,128)(2,1)}), bf16[256,4096]{1,0:T(8,128)(2,1)}) %all-gather.12.cloned.1.call-update) | async-done | bytes 2097168 | tf_op jit(solution)/shard_map/while/body/eval_jaxpr/all_gather | solution.py:76
  74.9 11.5 %convolution_convert_fusion.7 = bf16[256,4096]{1,0:T(8,128)(2,1)} fusion(bf16[2048,4096]{1,0:T(8,128)(2,1)} %get-tuple-element.638, bf16[256,4096]{1,0:T(8,128)(2,1)S(1)} %copy-done.6, s32[]{:T(128)} %get-tuple-element.634), kind=kOutput, calls=%fused_computation.2.clone.1 | convolution fusion | flops 4296015872 | bytes 19922948 | tf_op jit(solution)/shard_map/while/body/eval_jaxpr/dot_general | solution.py:78
  89.7 34.0 %reduce-scatter.7.cloned.1.call-done = bf16[128,4096]{1,0:T(8,128)(2,1)} async-done(((bf16[256,4096]{1,0:T(8,128)(2,1)}), bf16[128,4096]{1,0:T(8,128)(2,1)}) %reduce-scatter.7.cloned.1.call-update) | async-done | bytes 1048592 | tf_op jit(solution)/shard_map/while/body/eval_jaxpr/reduce_scatter | solution.py:81
  124.2 25.0 %all-reduce.2.cloned.1.call-done = bf16[128,1024]{1,0:T(8,128)(2,1)} async-done(((bf16[128,1024]{1,0:T(8,128)(2,1)}), bf16[128,1024]{1,0:T(8,128)(2,1)}) %all-reduce.2.cloned.1.call-update) | async-done | bytes 262160 | tf_op jit(solution)/shard_map/while/body/eval_jaxpr/psum | solution.py:94
  161.0 10.6 reduce-scatter.9.cloned.1.call-done
  176.8 21.4 %all-gather.14.cloned.1.call-done = bf16[256,2048]{1,0:T(8,128)(2,1)} async-done(((bf16[128,2048]{1,0:T(8,128)(2,1)}), bf16[256,2048]{1,0:T(8,128)(2,1)}) %all-gather.14.cloned.1.call-update) | async-done | bytes 1048592 | tf_op jit(solution)/shard_map/while/body/eval_jaxpr/all_gather | solution.py:138
  198.3 34.6 %all-gather.16.cloned.1.call-done = bf16[512,2048]{1,0:T(8,128)(2,1)} async-done(((bf16[256,2048]{1,0:T(8,128)(2,1)}), bf16[512,2048]{1,0:T(8,128)(2,1)}) %all-gather.16.cloned.1.call-update) | async-done | bytes 2097168 | tf_op jit(solution)/shard_map/while/body/eval_jaxpr/all_gather | solution.py:139
  235.7 8.3 convolution_convert_fusion.8
  244.0 16.2 %all_to_all.48 = bf16[2,128,2048]{2,1,0:T(8,128)(2,1)S(1)} all-to-all(bf16[2,128,2048]{2,1,0:T(8,128)(2,1)S(1)} %bitcast.141), channel_id=1, replica_groups=mesh['section'=4,'gx'=2,'gy'=2,'gz'=2] {'gy'}, dimensions={0} | all-to-all | bytes 2097152 | tf_op jit(solution)/shard_map/while/body/eval_jaxpr/all_to_all | solution.py:140
  261.3 7.6 reduce-scatter.11.cloned.1.call-done
  274.0 11.6 %collective-permute-done = bf16[128,2048]{1,0:T(8,128)(2,1)S(1)} collective-permute-done((bf16[128,2048]{1,0:T(8,128)(2,1)S(1)}, bf16[128,2048]{1,0:T(8,128)(2,1)S(1)}, u32[]{:S(2)}, u32[]{:S(2)}) %collective-permute-start) | collective-permute-done | bytes 524320 | tf_op jit(solution)/shard_map/while/body/eval_jaxpr/ppermute | solution.py:16
  287.5 11.1 all-gather.10.cloned.1.call-done
  307.6 34.4 %all-gather.12.cloned.1.call-done = bf16[256,4096]{1,0:T(8,128)(2,1)} async-done(((bf16[128,4096]{1,0:T(8,128)(2,1)}), bf16[256,4096]{1,0:T(8,128)(2,1)}) %all-gather.12.cloned.1.call-update) | async-done | bytes 2097168 | tf_op jit(solution)/shard_map/while/body/eval_jaxpr/all_gather | solution.py:76
  346.8 11.5 %convolution_convert_fusion.7 = bf16[256,4096]{1,0:T(8,128)(2,1)} fusion(bf16[2048,4096]{1,0:T(8,128)(2,1)} %get-tuple-element.638, bf16[256,4096]{1,0:T(8,128)(2,1)S(1)} %copy-done.6, s32[]{:T(128)} %get-tuple-element.634), kind=kOutput, calls=%fused_computation.2.clone.1 | convolution fusion | flops 4296015872 | bytes 19922948 | tf_op jit(solution)/shard_map/while/body/eval_jaxpr/dot_general | solution.py:78
  361.6 34.1 %reduce-scatter.7.cloned.1.call-done = bf16[128,4096]{1,0:T(8,128)(2,1)} async-done(((bf16[256,4096]{1,0:T(8,128)(2,1)}), bf16[128,4096]{1,0:T(8,128)(2,1)}) %reduce-scatter.7.cloned.1.call-update) | async-done | bytes 1048592 | tf_op jit(solution)/shard_map/while/body/eval_jaxpr/reduce_scatter | solution.py:81
  396.2 25.0 %all-reduce.2.cloned.1.call-done = bf16[128,1024]{1,0:T(8,128)(2,1)} async-done(((bf16[128,1024]{1,0:T(8,128)(2,1)}), bf16[128,1024]{1,0:T(8,128)(2,1)}) %all-reduce.2.cloned.1.call-update) | async-done | bytes 262160 | tf_op jit(solution)/shard_map/while/body/eval_jaxpr/psum | solution.py:94
  433.0 10.6 reduce-scatter.9.cloned.1.call-done
  448.8 21.4 %all-gather.14.cloned.1.call-done = bf16[256,2048]{1,0:T(8,128)(2,1)} async-done(((bf16[128,2048]{1,0:T(8,128)(2,1)}), bf16[256,2048]{1,0:T(8,128)(2,1)}) %all-gather.14.cloned.1.call-update) | async-done | bytes 1048592 | tf_op jit(solution)/shard_map/while/body/eval_jaxpr/all_gather | solution.py:138
  470.3 34.4 %all-gather.16.cloned.1.call-done = bf16[512,2048]{1,0:T(8,128)(2,1)} async-done(((bf16[256,2048]{1,0:T(8,128)(2,1)}), bf16[512,2048]{1,0:T(8,128)(2,1)}) %all-gather.16.cloned.1.call-update) | async-done | bytes 2097168 | tf_op jit(solution)/shard_map/while/body/eval_jaxpr/all_gather | solution.py:139
  507.6 8.3 convolution_convert_fusion.8
  515.9 16.2 %all_to_all.48 = bf16[2,128,2048]{2,1,0:T(8,128)(2,1)S(1)} all-to-all(bf16[2,128,2048]{2,1,0:T(8,128)(2,1)S(1)} %bitcast.141), channel_id=1, replica_groups=mesh['section'=4,'gx'=2,'gy'=2,'gz'=2] {'gy'}, dimensions={0} | all-to-all | bytes 2097152 | tf_op jit(solution)/shard_map/while/body/eval_jaxpr/all_to_all | solution.py:140
  533.1 7.6 reduce-scatter.11.cloned.1.call-done
  545.8 11.6 %collective-permute-done = bf16[128,2048]{1,0:T(8,128)(2,1)S(1)} collective-permute-done((bf16[128,2048]{1,0:T(8,128)(2,1)S(1)}, bf16[128,2048]{1,0:T(8,128)(2,1)S(1)}, u32[]{:S(2)}, u32[]{:S(2)}) %collective-permute-start) | collective-permute-done | bytes 524320 | tf_op jit(solution)/shard_map/while/body/eval_jaxpr/ppermute | solution.py:16
  559.3 11.4 %all-gather.10.cloned.1.call-done = bf16[128,4096]{1,0:T(8,128)(2,1)} async-done(((bf16[128,2048]{1,0:T(8,128)(2,1)}), bf16[128,4096]{1,0:T(8,128)(2,1)}) %all-gather.10.cloned.1.call-update) | async-done | bytes 1048592 | tf_op jit(solution)/shard_map/while/body/eval_jaxpr/all_gather | solution.py:162
  579.8 34.4 %all-gather.12.cloned.1.call-done = bf16[256,4096]{1,0:T(8,128)(2,1)} async-done(((bf16[128,4096]{1,0:T(8,128)(2,1)}), bf16[256,4096]{1,0:T(8,128)(2,1)}) %all-gather.12.cloned.1.call-update) | async-done | bytes 2097168 | tf_op jit(solution)/shard_map/while/body/eval_jaxpr/all_gather | solution.py:76
  618.9 11.5 %convolution_convert_fusion.7 = bf16[256,4096]{1,0:T(8,128)(2,1)} fusion(bf16[2048,4096]{1,0:T(8,128)(2,1)} %get-tuple-element.638, bf16[256,4096]{1,0:T(8,128)(2,1)S(1)} %copy-done.6, s32[]{:T(128)} %get-tuple-element.634), kind=kOutput, calls=%fused_computation.2.clone.1 | convolution fusion | flops 4296015872 | bytes 19922948 | tf_op jit(solution)/shard_map/while/body/eval_jaxpr/dot_general | solution.py:78
  633.7 34.1 %reduce-scatter.7.cloned.1.call-done = bf16[128,4096]{1,0:T(8,128)(2,1)} async-done(((bf16[256,4096]{1,0:T(8,128)(2,1)}), bf16[128,4096]{1,0:T(8,128)(2,1)}) %reduce-scatter.7.cloned.1.call-update) | async-done | bytes 1048592 | tf_op jit(solution)/shard_map/while/body/eval_jaxpr/reduce_scatter | solution.py:81
  668.3 25.1 %all-reduce.2.cloned.1.call-done = bf16[128,1024]{1,0:T(8,128)(2,1)} async-done(((bf16[128,1024]{1,0:T(8,128)(2,1)}), bf16[128,1024]{1,0:T(8,128)(2,1)}) %all-reduce.2.cloned.1.call-update) | async-done | bytes 262160 | tf_op jit(solution)/shard_map/while/body/eval_jaxpr/psum | solution.py:94
  705.3 10.6 reduce-scatter.9.cloned.1.call-done
  721.1 21.4 %all-gather.14.cloned.1.call-done = bf16[256,2048]{1,0:T(8,128)(2,1)} async-done(((bf16[128,2048]{1,0:T(8,128)(2,1)}), bf16[256,2048]{1,0:T(8,128)(2,1)}) %all-gather.14.cloned.1.call-update) | async-done | bytes 1048592 | tf_op jit(solution)/shard_map/while/body/eval_jaxpr/all_gather | solution.py:138
  742.6 34.4 %all-gather.16.cloned.1.call-done = bf16[512,2048]{1,0:T(8,128)(2,1)} async-done(((bf16[256,2048]{1,0:T(8,128)(2,1)}), bf16[512,2048]{1,0:T(8,128)(2,1)}) %all-gather.16.cloned.1.call-update) | async-done | bytes 2097168 | tf_op jit(solution)/shard_map/while/body/eval_jaxpr/all_gather | solution.py:139
  779.9 8.3 convolution_convert_fusion.8
  788.2 16.2 %all_to_all.48 = bf16[2,128,2048]{2,1,0:T(8,128)(2,1)S(1)} all-to-all(bf16[2,128,2048]{2,1,0:T(8,128)(2,1)S(1)} %bitcast.141), channel_id=1, replica_groups=mesh['section'=4,'gx'=2,'gy'=2,'gz'=2] {'gy'}, dimensions={0} | all-to-all | bytes 2097152 | tf_op jit(solution)/shard_map/while/body/eval_jaxpr/all_to_all | solution.py:140
  805.4 7.6 reduce-scatter.11.cloned.1.call-done
  818.1 11.6 %collective-permute-done = bf16[128,2048]{1,0:T(8,128)(2,1)S(1)} collective-permute-done((bf16[128,2048]{1,0:T(8,128)(2,1)S(1)}, bf16[128,2048]{1,0:T(8,128)(2,1)S(1)}, u32[]{:S(2)}, u32[]{:S(2)}) %collective-permute-start) | collective-permute-done | bytes 524320 | tf_op jit(solution)/shard_map/while/body/eval_jaxpr/ppermute | solution.py:16
  831.7 11.3 %all-gather.10.cloned.1.call-done = bf16[128,4096]{1,0:T(8,128)(2,1)} async-done(((bf16[128,2048]{1,0:T(8,128)(2,1)}), bf16[128,4096]{1,0:T(8,128)(2,1)}) %all-gather.10.cloned.1.call-update) | async-done | bytes 1048592 | tf_op jit(solution)/shard_map/while/body/eval_jaxpr/all_gather | solution.py:162
  852.1 34.4 %all-gather.12.cloned.1.call-done = bf16[256,4096]{1,0:T(8,128)(2,1)} async-done(((bf16[128,4096]{1,0:T(8,128)(2,1)}), bf16[256,4096]{1,0:T(8,128)(2,1)}) %all-gather.12.cloned.1.call-update) | async-done | bytes 2097168 | tf_op jit(solution)/shard_map/while/body/eval_jaxpr/all_gather | solution.py:76
  891.3 11.5 %convolution_convert_fusion.7 = bf16[256,4096]{1,0:T(8,128)(2,1)} fusion(bf16[2048,4096]{1,0:T(8,128)(2,1)} %get-tuple-element.638, bf16[256,4096]{1,0:T(8,128)(2,1)S(1)} %copy-done.6, s32[]{:T(128)} %get-tuple-element.634), kind=kOutput, calls=%fused_computation.2.clone.1 | convolution fusion | flops 4296015872 | bytes 19922948 | tf_op jit(solution)/shard_map/while/body/eval_jaxpr/dot_general | solution.py:78
  906.1 34.1 %reduce-scatter.7.cloned.1.call-done = bf16[128,4096]{1,0:T(8,128)(2,1)} async-done(((bf16[256,4096]{1,0:T(8,128)(2,1)}), bf16[128,4096]{1,0:T(8,128)(2,1)}) %reduce-scatter.7.cloned.1.call-update) | async-done | bytes 1048592 | tf_op jit(solution)/shard_map/while/body/eval_jaxpr/reduce_scatter | solution.py:81
  940.7 25.1 %all-reduce.2.cloned.1.call-done = bf16[128,1024]{1,0:T(8,128)(2,1)} async-done(((bf16[128,1024]{1,0:T(8,128)(2,1)}), bf16[128,1024]{1,0:T(8,128)(2,1)}) %all-reduce.2.cloned.1.call-update) | async-done | bytes 262160 | tf_op jit(solution)/shard_map/while/body/eval_jaxpr/psum | solution.py:94
  977.7 10.6 reduce-scatter.9.cloned.1.call-done
  993.4 21.4 %all-gather.14.cloned.1.call-done = bf16[256,2048]{1,0:T(8,128)(2,1)} async-done(((bf16[128,2048]{1,0:T(8,128)(2,1)}), bf16[256,2048]{1,0:T(8,128)(2,1)}) %all-gather.14.cloned.1.call-update) | async-done | bytes 1048592 | tf_op jit(solution)/shard_map/while/body/eval_jaxpr/all_gather | solution.py:138
  1014.9 34.6 %all-gather.16.cloned.1.call-done = bf16[512,2048]{1,0:T(8,128)(2,1)} async-done(((bf16[256,2048]{1,0:T(8,128)(2,1)}), bf16[512,2048]{1,0:T(8,128)(2,1)}) %all-gather.16.cloned.1.call-update) | async-done | bytes 2097168 | tf_op jit(solution)/shard_map/while/body/eval_jaxpr/all_gather | solution.py:139
  1052.3 8.3 convolution_convert_fusion.8
  1060.7 16.2 %all_to_all.48 = bf16[2,128,2048]{2,1,0:T(8,128)(2,1)S(1)} all-to-all(bf16[2,128,2048]{2,1,0:T(8,128)(2,1)S(1)} %bitcast.141), channel_id=1, replica_groups=mesh['section'=4,'gx'=2,'gy'=2,'gz'=2] {'gy'}, dimensions={0} | all-to-all | bytes 2097152 | tf_op jit(solution)/shard_map/while/body/eval_jaxpr/all_to_all | solution.py:140
  1090.6 11.6 %collective-permute-done = bf16[128,2048]{1,0:T(8,128)(2,1)S(1)} collective-permute-done((bf16[128,2048]{1,0:T(8,128)(2,1)S(1)}, bf16[128,2048]{1,0:T(8,128)(2,1)S(1)}, u32[]{:S(2)}, u32[]{:S(2)}) %collective-permute-start) | collective-permute-done | bytes 524320 | tf_op jit(solution)/shard_map/while/body/eval_jaxpr/ppermute | solution.py:16
  (252 shorter events, 195.9 us)
Async XLA Ops:
  12.5 14.1 %all-gather.10.cloned.1.call-start = ((), (), s32[]{:S(2)}) async-start(), calls=%async_computation.5 | async-start | bytes 1572864 | tf_op jit(solution)/shard_map/while/body/eval_jaxpr/all_gather | solution.py:162
  14.5 55.6 %all-gather.12.cloned.1.call-start = ((), (), s32[]{:S(2)}) async-start(), calls=%async_computation.6 | async-start | bytes 3145728 | tf_op jit(solution)/shard_map/while/body/eval_jaxpr/all_gather | solution.py:76
  35.7 54.0 %reduce-scatter.5.cloned.1.call-start = ((), (), s32[]{:S(2)}) async-start(), calls=%async_computation.7 | async-start | bytes 786432 | tf_op jit(solution)/shard_map/while/body/eval_jaxpr/reduce_scatter | solution.py:84
  70.1 4.8 copy-start.6
  74.9 48.8 %reduce-scatter.7.cloned.1.call-start = ((), (), s32[]{:S(2)}) async-start(), calls=%async_computation.9 | async-start | bytes 3145728 | tf_op jit(solution)/shard_map/while/body/eval_jaxpr/reduce_scatter | solution.py:81
  86.5 62.7 %all-reduce.2.cloned.1.call-start = ((), (), s32[]{:S(2)}) async-start(), calls=%async_computation.8 | async-start | bytes 524288 | tf_op jit(solution)/shard_map/while/body/eval_jaxpr/psum | solution.py:94
  89.7 82.0 %reduce-scatter.9.cloned.1.call-start = ((), (), s32[]{:S(2)}) async-start(), calls=%async_computation.10 | async-start | bytes 1572864 | tf_op jit(solution)/shard_map/while/body/eval_jaxpr/reduce_scatter | solution.py:89
  123.7 74.5 %all-gather.14.cloned.1.call-start = ((), (), s32[]{:S(2)}) async-start(), calls=%async_computation.11 | async-start | bytes 1572864 | tf_op jit(solution)/shard_map/while/body/eval_jaxpr/all_gather | solution.py:138
  176.7 56.1 %all-gather.16.cloned.1.call-start = ((), (), s32[]{:S(2)}) async-start(), calls=%async_computation.12 | async-start | bytes 3145728 | tf_op jit(solution)/shard_map/while/body/eval_jaxpr/all_gather | solution.py:139
  198.2 70.7 %reduce-scatter.11.cloned.1.call-start = ((), (), s32[]{:S(2)}) async-start(), calls=%async_computation.13 | async-start | bytes 1572864 | tf_op jit(solution)/shard_map/while/body/eval_jaxpr/reduce_scatter | solution.py:163
  260.2 8.7 copy-start.2
  270.2 15.3 %collective-permute-start = (bf16[128,2048]{1,0:T(8,128)(2,1)S(1)}, bf16[128,2048]{1,0:T(8,128)(2,1)S(1)}, u32[]{:S(2)}, u32[]{:S(2)}) collective-permute-start(bf16[128,2048]{1,0:T(8,128)(2,1)S(1)} %get-tuple-element.592), channel_id=1, source_target_pairs={{0,8},{8,16},{16,24},{1,9},{9,17},{17,25},{2,10},{10,18},{18,26},{... | collective-permute-start | bytes 1572872 | tf_op jit(solution)/shard_map/while/body/eval_jaxpr/ppermute | solution.py:16
  285.5 13.0 %all-gather.10.cloned.1.call-start = ((), (), s32[]{:S(2)}) async-start(), calls=%async_computation.5 | async-start | bytes 1572864 | tf_op jit(solution)/shard_map/while/body/eval_jaxpr/all_gather | solution.py:162
  287.4 54.6 %all-gather.12.cloned.1.call-start = ((), (), s32[]{:S(2)}) async-start(), calls=%async_computation.6 | async-start | bytes 3145728 | tf_op jit(solution)/shard_map/while/body/eval_jaxpr/all_gather | solution.py:76
  307.6 54.0 %reduce-scatter.5.cloned.1.call-start = ((), (), s32[]{:S(2)}) async-start(), calls=%async_computation.7 | async-start | bytes 786432 | tf_op jit(solution)/shard_map/while/body/eval_jaxpr/reduce_scatter | solution.py:84
  342.0 4.8 copy-start.6
  346.7 49.0 %reduce-scatter.7.cloned.1.call-start = ((), (), s32[]{:S(2)}) async-start(), calls=%async_computation.9 | async-start | bytes 3145728 | tf_op jit(solution)/shard_map/while/body/eval_jaxpr/reduce_scatter | solution.py:81
  358.3 62.8 %all-reduce.2.cloned.1.call-start = ((), (), s32[]{:S(2)}) async-start(), calls=%async_computation.8 | async-start | bytes 524288 | tf_op jit(solution)/shard_map/while/body/eval_jaxpr/psum | solution.py:94
  361.5 82.1 %reduce-scatter.9.cloned.1.call-start = ((), (), s32[]{:S(2)}) async-start(), calls=%async_computation.10 | async-start | bytes 1572864 | tf_op jit(solution)/shard_map/while/body/eval_jaxpr/reduce_scatter | solution.py:89
  395.7 74.5 %all-gather.14.cloned.1.call-start = ((), (), s32[]{:S(2)}) async-start(), calls=%async_computation.11 | async-start | bytes 1572864 | tf_op jit(solution)/shard_map/while/body/eval_jaxpr/all_gather | solution.py:138
  448.7 56.0 %all-gather.16.cloned.1.call-start = ((), (), s32[]{:S(2)}) async-start(), calls=%async_computation.12 | async-start | bytes 3145728 | tf_op jit(solution)/shard_map/while/body/eval_jaxpr/all_gather | solution.py:139
  470.2 70.5 %reduce-scatter.11.cloned.1.call-start = ((), (), s32[]{:S(2)}) async-start(), calls=%async_computation.13 | async-start | bytes 1572864 | tf_op jit(solution)/shard_map/while/body/eval_jaxpr/reduce_scatter | solution.py:163
  532.0 8.7 copy-start.2
  542.1 15.3 %collective-permute-start = (bf16[128,2048]{1,0:T(8,128)(2,1)S(1)}, bf16[128,2048]{1,0:T(8,128)(2,1)S(1)}, u32[]{:S(2)}, u32[]{:S(2)}) collective-permute-start(bf16[128,2048]{1,0:T(8,128)(2,1)S(1)} %get-tuple-element.592), channel_id=1, source_target_pairs={{0,8},{8,16},{16,24},{1,9},{9,17},{17,25},{2,10},{10,18},{18,26},{... | collective-permute-start | bytes 1572872 | tf_op jit(solution)/shard_map/while/body/eval_jaxpr/ppermute | solution.py:16
  557.4 13.3 %all-gather.10.cloned.1.call-start = ((), (), s32[]{:S(2)}) async-start(), calls=%async_computation.5 | async-start | bytes 1572864 | tf_op jit(solution)/shard_map/while/body/eval_jaxpr/all_gather | solution.py:162
  559.3 54.9 %all-gather.12.cloned.1.call-start = ((), (), s32[]{:S(2)}) async-start(), calls=%async_computation.6 | async-start | bytes 3145728 | tf_op jit(solution)/shard_map/while/body/eval_jaxpr/all_gather | solution.py:76
  579.7 54.0 %reduce-scatter.5.cloned.1.call-start = ((), (), s32[]{:S(2)}) async-start(), calls=%async_computation.7 | async-start | bytes 786432 | tf_op jit(solution)/shard_map/while/body/eval_jaxpr/reduce_scatter | solution.py:84
  614.2 4.8 copy-start.6
  618.9 49.0 %reduce-scatter.7.cloned.1.call-start = ((), (), s32[]{:S(2)}) async-start(), calls=%async_computation.9 | async-start | bytes 3145728 | tf_op jit(solution)/shard_map/while/body/eval_jaxpr/reduce_scatter | solution.py:81
  630.5 63.0 %all-reduce.2.cloned.1.call-start = ((), (), s32[]{:S(2)}) async-start(), calls=%async_computation.8 | async-start | bytes 524288 | tf_op jit(solution)/shard_map/while/body/eval_jaxpr/psum | solution.py:94
  633.7 82.3 %reduce-scatter.9.cloned.1.call-start = ((), (), s32[]{:S(2)}) async-start(), calls=%async_computation.10 | async-start | bytes 1572864 | tf_op jit(solution)/shard_map/while/body/eval_jaxpr/reduce_scatter | solution.py:89
  667.9 74.6 %all-gather.14.cloned.1.call-start = ((), (), s32[]{:S(2)}) async-start(), calls=%async_computation.11 | async-start | bytes 1572864 | tf_op jit(solution)/shard_map/while/body/eval_jaxpr/all_gather | solution.py:138
  721.1 56.0 %all-gather.16.cloned.1.call-start = ((), (), s32[]{:S(2)}) async-start(), calls=%async_computation.12 | async-start | bytes 3145728 | tf_op jit(solution)/shard_map/while/body/eval_jaxpr/all_gather | solution.py:139
  742.5 70.5 %reduce-scatter.11.cloned.1.call-start = ((), (), s32[]{:S(2)}) async-start(), calls=%async_computation.13 | async-start | bytes 1572864 | tf_op jit(solution)/shard_map/while/body/eval_jaxpr/reduce_scatter | solution.py:163
  804.3 8.7 copy-start.2
  814.4 15.3 %collective-permute-start = (bf16[128,2048]{1,0:T(8,128)(2,1)S(1)}, bf16[128,2048]{1,0:T(8,128)(2,1)S(1)}, u32[]{:S(2)}, u32[]{:S(2)}) collective-permute-start(bf16[128,2048]{1,0:T(8,128)(2,1)S(1)} %get-tuple-element.592), channel_id=1, source_target_pairs={{0,8},{8,16},{16,24},{1,9},{9,17},{17,25},{2,10},{10,18},{18,26},{... | collective-permute-start | bytes 1572872 | tf_op jit(solution)/shard_map/while/body/eval_jaxpr/ppermute | solution.py:16
  829.7 13.3 %all-gather.10.cloned.1.call-start = ((), (), s32[]{:S(2)}) async-start(), calls=%async_computation.5 | async-start | bytes 1572864 | tf_op jit(solution)/shard_map/while/body/eval_jaxpr/all_gather | solution.py:162
  831.6 54.8 %all-gather.12.cloned.1.call-start = ((), (), s32[]{:S(2)}) async-start(), calls=%async_computation.6 | async-start | bytes 3145728 | tf_op jit(solution)/shard_map/while/body/eval_jaxpr/all_gather | solution.py:76
  852.0 54.0 %reduce-scatter.5.cloned.1.call-start = ((), (), s32[]{:S(2)}) async-start(), calls=%async_computation.7 | async-start | bytes 786432 | tf_op jit(solution)/shard_map/while/body/eval_jaxpr/reduce_scatter | solution.py:84
  886.5 4.8 copy-start.6
  891.2 49.0 %reduce-scatter.7.cloned.1.call-start = ((), (), s32[]{:S(2)}) async-start(), calls=%async_computation.9 | async-start | bytes 3145728 | tf_op jit(solution)/shard_map/while/body/eval_jaxpr/reduce_scatter | solution.py:81
  902.8 63.0 %all-reduce.2.cloned.1.call-start = ((), (), s32[]{:S(2)}) async-start(), calls=%async_computation.8 | async-start | bytes 524288 | tf_op jit(solution)/shard_map/while/body/eval_jaxpr/psum | solution.py:94
  906.0 82.3 %reduce-scatter.9.cloned.1.call-start = ((), (), s32[]{:S(2)}) async-start(), calls=%async_computation.10 | async-start | bytes 1572864 | tf_op jit(solution)/shard_map/while/body/eval_jaxpr/reduce_scatter | solution.py:89
  940.2 74.6 %all-gather.14.cloned.1.call-start = ((), (), s32[]{:S(2)}) async-start(), calls=%async_computation.11 | async-start | bytes 1572864 | tf_op jit(solution)/shard_map/while/body/eval_jaxpr/all_gather | solution.py:138
  993.4 56.1 %all-gather.16.cloned.1.call-start = ((), (), s32[]{:S(2)}) async-start(), calls=%async_computation.12 | async-start | bytes 3145728 | tf_op jit(solution)/shard_map/while/body/eval_jaxpr/all_gather | solution.py:139
  1014.9 70.7 %reduce-scatter.11.cloned.1.call-start = ((), (), s32[]{:S(2)}) async-start(), calls=%async_computation.13 | async-start | bytes 1572864 | tf_op jit(solution)/shard_map/while/body/eval_jaxpr/reduce_scatter | solution.py:163
  1076.8 8.7 copy-start.2
  1086.9 15.3 %collective-permute-start = (bf16[128,2048]{1,0:T(8,128)(2,1)S(1)}, bf16[128,2048]{1,0:T(8,128)(2,1)S(1)}, u32[]{:S(2)}, u32[]{:S(2)}) collective-permute-start(bf16[128,2048]{1,0:T(8,128)(2,1)S(1)} %get-tuple-element.592), channel_id=1, source_target_pairs={{0,8},{8,16},{16,24},{1,9},{9,17},{17,25},{2,10},{10,18},{18,26},{... | collective-permute-start | bytes 1572872 | tf_op jit(solution)/shard_map/while/body/eval_jaxpr/ppermute | solution.py:16
  (5 other events, 7.8 us)
Sparse Core Ops, SparseCore 0:
  14.9 11.7 all-gather.9
  35.8 34.2 all-gather.11
  75.0 14.6 reduce-scatter.4
  91.8 31.8 reduce-scatter.6
  125.8 23.2 all-reduce.1
  151.2 20.3 reduce-scatter.8
  176.9 21.2 all-gather.13
  199.7 33.0 all-gather.15
  261.4 7.4 reduce-scatter.10
  287.5 10.9 all-gather.9
  307.7 34.2 all-gather.11
  346.8 14.6 reduce-scatter.4
  363.8 31.8 reduce-scatter.6
  397.8 23.2 all-reduce.1
  423.2 20.3 reduce-scatter.8
  448.9 21.2 all-gather.13
  471.6 33.0 all-gather.15
  533.2 7.4 reduce-scatter.10
  559.7 10.9 all-gather.9
  579.8 34.2 all-gather.11
  619.0 14.6 reduce-scatter.4
  635.9 31.8 reduce-scatter.6
  670.1 23.2 all-reduce.1
  695.6 20.3 reduce-scatter.8
  721.2 21.2 all-gather.13
  743.9 33.0 all-gather.15
  805.5 7.4 reduce-scatter.10
  832.1 10.9 all-gather.9
  852.2 34.2 all-gather.11
  891.3 14.6 reduce-scatter.4
  908.2 31.8 reduce-scatter.6
  942.5 23.2 all-reduce.1
  967.9 20.3 reduce-scatter.8
  993.5 21.2 all-gather.13
  1016.4 33.0 all-gather.15
  1078.0 7.4 reduce-scatter.10
